TPU v7x, 32 devices: a whole 2x2x4 slice. The times are simulated.
32 devices in a mesh: groups: 2 (over x), blk: 16 (over z, y, core).
Axes of the slice: x: 2, y: 2, z: 4, core: 2. Of those that a mesh axis runs over, the one named last changes fastest.
Arguments:
- coords: float32 [32, 24576], P(None, ('groups', 'blk')), parts along dimension 1, may hold values from -6 to 6
- alpha: float32 [24576], P(('groups', 'blk')), parts along dimension 0, may hold values from -6 to 6
- probe_solves: float32 [15, 24576], P(None, ('groups', 'blk')), parts along dimension 1, may hold values from -6 to 6
- probes: float32 [15, 24576], P(None, ('groups', 'blk')), parts along dimension 1, may hold values from -6 to 6
- lengthscale: float32 [32], replicated, may hold values from 4 to 12
Outputs:
- grad: float32 [32, 24576], P(None, ('groups', 'blk')), parts along dimension 1
There are 2 independent parts, one for each index of `groups`. A program takes and returns all parts, laid end to end along the dimension named above; an argument that names none is the same for every part. Nothing has to cross between parts.
All inputs are finite; a program needn't handle non-finite values.
Results may differ from a plain program's by a relative error of at most 0.00014.
Values sent between devices are 32-bit elements; how exact they have to be, the bound alone decides.
A program may use at most 64 MiB of HBM per device.

v0:
```python
import jax
import jax.numpy as jnp
from jax import lax
from jax.sharding import PartitionSpec as P

root_five = 5.0**0.5


def shifted(value, axis, steps):
    count = lax.axis_size(axis)
    pairs = [(source, (source + steps) % count) for source in range(count)]
    return lax.ppermute(value, axis, pairs)


def tile_terms(own_scaled, own_table, vis_scaled, vis_table):
    probe_count = (own_table.shape[0] - 1) // 2
    half_inv = 1.0 / (2.0 * probe_count)
    left_rows = jnp.concatenate([own_table[:1], -half_inv * own_table[1:]], 0)
    right_rows = jnp.concatenate(
        [vis_table[:1], vis_table[1 + probe_count :], vis_table[1 : 1 + probe_count]], 0
    )
    contract_first = (((0,), (0,)), ((), ()))
    inner = lax.dot_general(
        own_scaled,
        vis_scaled,
        contract_first,
        precision=lax.Precision.HIGHEST,
        preferred_element_type=jnp.float32,
    )
    own_square = jnp.sum(own_scaled * own_scaled, 0)
    vis_square = jnp.sum(vis_scaled * vis_scaled, 0)
    distance = own_square[:, None] + vis_square[None, :] - 2.0 * inner
    radius = jnp.sqrt(jnp.maximum(distance, 0.0))
    profile = (1.0 + root_five * radius) * jnp.exp(-root_five * radius)
    coupling = lax.dot_general(
        left_rows,
        right_rows,
        contract_first,
        precision=lax.Precision.HIGHEST,
        preferred_element_type=jnp.float32,
    )
    weighted = coupling * profile
    row_part = own_scaled * jnp.sum(weighted, 1)[None, :] - lax.dot_general(
        vis_scaled,
        weighted,
        (((1,), (1,)), ((), ())),
        precision=lax.Precision.HIGHEST,
        preferred_element_type=jnp.float32,
    )
    col_part = vis_scaled * jnp.sum(weighted, 0)[None, :] - jnp.dot(
        own_scaled, weighted, precision=lax.Precision.HIGHEST, preferred_element_type=jnp.float32
    )
    return (row_part, col_part)


def on_device(coords, alpha, probe_solves, probes, lengthscale):
    scaled = coords / lengthscale[:, None]
    table = jnp.concatenate([alpha[None], probe_solves, probes], 0)
    step_count = lax.axis_size("blk") // 4
    vis_scaled, vis_table = shifted((scaled, table), "blk", -1)
    zero_field = jnp.zeros(scaled.shape, jnp.float32)

    def carry_step(index, state):
        cur_scaled, cur_table, col_acc, row_total = state
        row_part, col_part = tile_terms(scaled, table, cur_scaled, cur_table)
        moved = shifted((cur_scaled, cur_table, col_acc + col_part), "blk", -1)
        return (moved[0], moved[1], moved[2], row_total + row_part)

    cur_scaled, cur_table, col_acc, row_total = lax.fori_loop(
        0, step_count - 1, carry_step, (vis_scaled, vis_table, zero_field, zero_field)
    )
    row_part, col_part = tile_terms(scaled, table, cur_scaled, cur_table)
    row_total = row_total + row_part
    col_total = shifted(col_acc + col_part, "blk", step_count)
    return -(5.0 / 3.0) / lengthscale[:, None] * (row_total + col_total)


def solution(mesh):
    return jax.shard_map(
        on_device,
        mesh=mesh,
        in_specs=(
            P(None, ("groups", "blk")),
            P(("groups", "blk")),
            P(None, ("groups", "blk")),
            P(None, ("groups", "blk")),
            P(),
        ),
        out_specs=P(None, ("groups", "blk")),
        check_vma=False,
    )
```

profile of v0, /device:TPU:1, one launch (start us, length us, event | category | flops | bytes accessed | tf_op | source)
XLA Modules:
  0.0 68.4 jit_solution(11254730001357348302)
XLA Ops:
  0.0 1.0 %multiply_reduce_fusion.2 = (f32[768]{0:T(1024)S(1)}, f32[32,768]{1,0:T(8,128)S(1)}) fusion(f32[32,768]{1,0:T(8,128)} %param.7, f32[32]{0:T(128)} %param.11), kind=kLoop, calls=%fused_computation.35 | loop fusion | flops 72960 | bytes 199808 | tf_op jit(solution)/shard_map/while/body/eval_jaxpr/reduce_sum | solution.py:30
  1.0 0.1 collective-permute-start.3
  1.1 0.7 %broadcast_in_dim.4 = f32[1,768]{1,0:T(1,128)S(1)} reshape(f32[768]{0:T(1024)} %param.8) | data formatting | bytes 6144 | tf_op jit(solution)/shard_map/broadcast_in_dim | solution.py:58
  1.8 0.8 %fusion.14 = f32[31,768]{1,0:T(8,128)S(1)} fusion(f32[1,768]{1,0:T(1,128)S(1)} %broadcast_in_dim.4, f32[15,768]{1,0:T(8,128)} %param.10, f32[15,768]{1,0:T(8,128)} %param.9), kind=kLoop, calls=%fused_computation.23 | loop fusion | flops 47616 | bytes 190464 | tf_op jit(solution)/shard_map/concatenate | solution.py:58
  2.6 5.5 %collective-permute-start.4 = (f32[31,768]{1,0:T(8,128)S(1)}, f32[31,768]{1,0:T(8,128)S(1)}, u32[]{:S(2)}, u32[]{:S(2)}) collective-permute-start(f32[31,768]{1,0:T(8,128)S(1)} %fusion.14), channel_id=1, source_target_pairs={{0,15},{1,0},{2,1},{3,2},{4,3},{5,4},{6,5},{7,6},{8,7},{9,8},{10,9... | collective-permute-start | bytes 285704 | tf_op jit(solution)/shard_map/ppermute | solution.py:12
  8.1 0.7 broadcast_divide_fusion.1
  8.8 0.8 %maximum_multiply_fusion = f32[30,768]{1,0:T(8,128)S(1)} fusion(f32[15,768]{1,0:T(8,128)} %param.10, f32[15,768]{1,0:T(8,128)} %param.9), kind=kLoop, calls=%fused_computation.25 | loop fusion | flops 46080 | bytes 184320 | tf_op jit(solution)/shard_map/mul | solution.py:18
  9.6 0.0 collective-permute-done.4
  9.6 0.0 collective-permute-done.3
  9.7 45.6 %while.19 = (s32[]{:T(128)}, f32[32,768]{1,0:T(8,128)S(1)}, f32[31,768]{1,0:T(8,128)S(1)}, f32[32,768]{1,0:T(8,128)S(1)}, f32[32,768]{1,0:T(8,128)S(1)}, /*index...) while((s32[]{:T(128)}, f32[32,768]{1,0:T(8,128)S(1)}, ...), condition=%wide.region_5.0_spmd.clone, body=%wide.region_1.5_spmd.clone.sunk | while | flops 905693184 | bytes 15019247 | solution.py:69
  9.7 1.4 %collective-permute-start = (f32[32,768]{1,0:T(8,128)S(1)}, f32[32,768]{1,0:T(8,128)S(1)}, u32[]{:S(2)}, u32[]{:S(2)}) collective-permute-start(f32[32,768]{1,0:T(8,128)S(1)} %copy.12), channel_id=1, source_target_pairs={{0,15},{1,0},{2,1},{3,2},{4,3},{5,4},{6,5},{7,6},{8,7},{9,8},{10,9... | collective-permute-start | bytes 294920 | tf_op jit(solution)/shard_map/while/body/eval_jaxpr/ppermute | solution.py:12
  11.1 4.6 %collective-permute-start.1 = (f32[31,768]{1,0:T(8,128)S(1)}, f32[31,768]{1,0:T(8,128)S(1)}, u32[]{:S(2)}, u32[]{:S(2)}) collective-permute-start(f32[31,768]{1,0:T(8,128)S(1)} %copy.13), channel_id=1, source_target_pairs={{0,15},{1,0},{2,1},{3,2},{4,3},{5,4},{6,5},{7,6},{8,7},{9,8},{10,9... | collective-permute-start | bytes 285704 | tf_op jit(solution)/shard_map/while/body/eval_jaxpr/ppermute | solution.py:12
  15.8 2.1 %fusion.62 = f32[768,768]{1,0:T(8,128)S(1)} fusion(f32[30,768]{1,0:T(8,128)S(1)} %slice_multiply_fusion.2, f32[1,768]{1,0:T(1,128)S(1)} %get-tuple-element.264, f32[15,768]{1,0:T(8,128)S(1)} %get-tuple-element.231, f32[15,768]{1,0:T(8,128)S(1)} %get-tuple-element.232, f32[1,768]{1,0:T(1,128)S(1)} %slice.50), kind=kOutput, calls=%fused_computation.7.clone.1 | convolution fusion | flops 219485952 | bytes 2549760 | tf_op jit(solution)/shard_map/while/body/eval_jaxpr/dot_general | solution.py:35
  17.8 3.5 %fusion.63 = (f32[768]{0:T(1024)S(1)}, f32[768]{0:T(1024)S(1)}, f32[768,768]{1,0:T(8,128)S(1)}) fusion(f32[768,768]{1,0:T(8,128)S(1)} %fusion.62, f32[32,768]{1,0:T(8,128)S(1)} %get-tuple-element.266, f32[32,768]{1,0:T(8,128)S(1)} %copy.12, f32[768]{0:T(1024)S(1)} %multiply_reduce_fusion.4, f32[768]{0:T(1024)S(1)} %get-tuple-element.265), kind=kOutput, calls=%fused_computation.39.clone.1 | convolution fusion | flops 232978944 | bytes 4927488 | tf_op jit(solution)/shard_map/while/body/eval_jaxpr/dot_general | solution.py:23
  21.3 1.5 %fusion.64 = f32[32,768]{1,0:T(8,128)S(1)} fusion(f32[32,768]{1,0:T(8,128)S(1)} %get-tuple-element.250, f32[768,768]{1,0:T(8,128)S(1)} %get-tuple-element.233, f32[32,768]{1,0:T(8,128)S(1)} %get-tuple-element.266, f32[32,768]{1,0:T(8,128)S(1)} %copy.12, f32[768]{0:T(1024)S(1)} %get-tuple-element.234), kind=kOutput, calls=%fused_computation.5.clone.1 | convolution fusion | flops 226566144 | bytes 2755584 | tf_op jit(solution)/shard_map/while/body/eval_jaxpr/dot_general | solution.py:50
  22.9 0.1 collective-permute-start.2
  22.9 2.2 %fusion.65 = f32[32,768]{1,0:T(8,128)S(1)} fusion(f32[768,768]{1,0:T(8,128)S(1)} %get-tuple-element.233, f32[32,768]{1,0:T(8,128)S(1)} %copy.12, f32[32,768]{1,0:T(8,128)S(1)} %get-tuple-element.251, f32[32,768]{1,0:T(8,128)S(1)} %get-tuple-element.266, f32[768]{0:T(1024)S(1)} %get-tuple-element.235, pred[]{:T(512)S(6)} %compare.3), kind=kOutput, calls=%fused_computation.6.clone.1 | convolution fusion | flops 226590720 | bytes 2755585 | tf_op jit(solution)/shard_map/while/body/eval_jaxpr/dot_general | solution.py:43
  25.2 0.0 collective-permute-done.1
  25.2 1.8 %collective-permute-done.2 = f32[32,768]{1,0:T(8,128)S(1)} collective-permute-done((f32[32,768]{1,0:T(8,128)S(1)}, f32[32,768]{1,0:T(8,128)S(1)}, u32[]{:S(2)}, u32[]{:S(2)}) %collective-permute-start.2) | collective-permute-done | bytes 98336 | tf_op jit(solution)/shard_map/while/body/eval_jaxpr/ppermute | solution.py:12
  27.0 0.0 collective-permute-done
  27.0 0.1 collective-permute-start
  27.1 2.8 %collective-permute-start.1 = (f32[31,768]{1,0:T(8,128)S(1)}, f32[31,768]{1,0:T(8,128)S(1)}, u32[]{:S(2)}, u32[]{:S(2)}) collective-permute-start(f32[31,768]{1,0:T(8,128)S(1)} %copy.13), channel_id=1, source_target_pairs={{0,15},{1,0},{2,1},{3,2},{4,3},{5,4},{6,5},{7,6},{8,7},{9,8},{10,9... | collective-permute-start | bytes 285704 | tf_op jit(solution)/shard_map/while/body/eval_jaxpr/ppermute | solution.py:12
  29.9 2.1 %fusion.62 = f32[768,768]{1,0:T(8,128)S(1)} fusion(f32[30,768]{1,0:T(8,128)S(1)} %slice_multiply_fusion.2, f32[1,768]{1,0:T(1,128)S(1)} %get-tuple-element.264, f32[15,768]{1,0:T(8,128)S(1)} %get-tuple-element.231, f32[15,768]{1,0:T(8,128)S(1)} %get-tuple-element.232, f32[1,768]{1,0:T(1,128)S(1)} %slice.50), kind=kOutput, calls=%fused_computation.7.clone.1 | convolution fusion | flops 219485952 | bytes 2549760 | tf_op jit(solution)/shard_map/while/body/eval_jaxpr/dot_general | solution.py:35
  32.0 3.5 %fusion.63 = (f32[768]{0:T(1024)S(1)}, f32[768]{0:T(1024)S(1)}, f32[768,768]{1,0:T(8,128)S(1)}) fusion(f32[768,768]{1,0:T(8,128)S(1)} %fusion.62, f32[32,768]{1,0:T(8,128)S(1)} %get-tuple-element.266, f32[32,768]{1,0:T(8,128)S(1)} %copy.12, f32[768]{0:T(1024)S(1)} %multiply_reduce_fusion.4, f32[768]{0:T(1024)S(1)} %get-tuple-element.265), kind=kOutput, calls=%fused_computation.39.clone.1 | convolution fusion | flops 232978944 | bytes 4927488 | tf_op jit(solution)/shard_map/while/body/eval_jaxpr/dot_general | solution.py:23
  35.5 1.5 %fusion.64 = f32[32,768]{1,0:T(8,128)S(1)} fusion(f32[32,768]{1,0:T(8,128)S(1)} %get-tuple-element.250, f32[768,768]{1,0:T(8,128)S(1)} %get-tuple-element.233, f32[32,768]{1,0:T(8,128)S(1)} %get-tuple-element.266, f32[32,768]{1,0:T(8,128)S(1)} %copy.12, f32[768]{0:T(1024)S(1)} %get-tuple-element.234), kind=kOutput, calls=%fused_computation.5.clone.1 | convolution fusion | flops 226566144 | bytes 2755584 | tf_op jit(solution)/shard_map/while/body/eval_jaxpr/dot_general | solution.py:50
  37.0 0.1 collective-permute-start.2
  37.1 2.2 %fusion.65 = f32[32,768]{1,0:T(8,128)S(1)} fusion(f32[768,768]{1,0:T(8,128)S(1)} %get-tuple-element.233, f32[32,768]{1,0:T(8,128)S(1)} %copy.12, f32[32,768]{1,0:T(8,128)S(1)} %get-tuple-element.251, f32[32,768]{1,0:T(8,128)S(1)} %get-tuple-element.266, f32[768]{0:T(1024)S(1)} %get-tuple-element.235, pred[]{:T(512)S(6)} %compare.3), kind=kOutput, calls=%fused_computation.6.clone.1 | convolution fusion | flops 226590720 | bytes 2755585 | tf_op jit(solution)/shard_map/while/body/eval_jaxpr/dot_general | solution.py:43
  39.3 0.0 collective-permute-done.1
  39.3 1.8 %collective-permute-done.2 = f32[32,768]{1,0:T(8,128)S(1)} collective-permute-done((f32[32,768]{1,0:T(8,128)S(1)}, f32[32,768]{1,0:T(8,128)S(1)}, u32[]{:S(2)}, u32[]{:S(2)}) %collective-permute-start.2) | collective-permute-done | bytes 98336 | tf_op jit(solution)/shard_map/while/body/eval_jaxpr/ppermute | solution.py:12
  41.1 0.0 collective-permute-done
  41.1 0.1 collective-permute-start
  41.2 2.8 %collective-permute-start.1 = (f32[31,768]{1,0:T(8,128)S(1)}, f32[31,768]{1,0:T(8,128)S(1)}, u32[]{:S(2)}, u32[]{:S(2)}) collective-permute-start(f32[31,768]{1,0:T(8,128)S(1)} %copy.13), channel_id=1, source_target_pairs={{0,15},{1,0},{2,1},{3,2},{4,3},{5,4},{6,5},{7,6},{8,7},{9,8},{10,9... | collective-permute-start | bytes 285704 | tf_op jit(solution)/shard_map/while/body/eval_jaxpr/ppermute | solution.py:12
  44.0 2.1 %fusion.62 = f32[768,768]{1,0:T(8,128)S(1)} fusion(f32[30,768]{1,0:T(8,128)S(1)} %slice_multiply_fusion.2, f32[1,768]{1,0:T(1,128)S(1)} %get-tuple-element.264, f32[15,768]{1,0:T(8,128)S(1)} %get-tuple-element.231, f32[15,768]{1,0:T(8,128)S(1)} %get-tuple-element.232, f32[1,768]{1,0:T(1,128)S(1)} %slice.50), kind=kOutput, calls=%fused_computation.7.clone.1 | convolution fusion | flops 219485952 | bytes 2549760 | tf_op jit(solution)/shard_map/while/body/eval_jaxpr/dot_general | solution.py:35
  46.1 3.5 %fusion.63 = (f32[768]{0:T(1024)S(1)}, f32[768]{0:T(1024)S(1)}, f32[768,768]{1,0:T(8,128)S(1)}) fusion(f32[768,768]{1,0:T(8,128)S(1)} %fusion.62, f32[32,768]{1,0:T(8,128)S(1)} %get-tuple-element.266, f32[32,768]{1,0:T(8,128)S(1)} %copy.12, f32[768]{0:T(1024)S(1)} %multiply_reduce_fusion.4, f32[768]{0:T(1024)S(1)} %get-tuple-element.265), kind=kOutput, calls=%fused_computation.39.clone.1 | convolution fusion | flops 232978944 | bytes 4927488 | tf_op jit(solution)/shard_map/while/body/eval_jaxpr/dot_general | solution.py:23
  49.6 1.5 %fusion.64 = f32[32,768]{1,0:T(8,128)S(1)} fusion(f32[32,768]{1,0:T(8,128)S(1)} %get-tuple-element.250, f32[768,768]{1,0:T(8,128)S(1)} %get-tuple-element.233, f32[32,768]{1,0:T(8,128)S(1)} %get-tuple-element.266, f32[32,768]{1,0:T(8,128)S(1)} %copy.12, f32[768]{0:T(1024)S(1)} %get-tuple-element.234), kind=kOutput, calls=%fused_computation.5.clone.1 | convolution fusion | flops 226566144 | bytes 2755584 | tf_op jit(solution)/shard_map/while/body/eval_jaxpr/dot_general | solution.py:50
  51.2 0.1 collective-permute-start.2
  51.2 2.2 %fusion.65 = f32[32,768]{1,0:T(8,128)S(1)} fusion(f32[768,768]{1,0:T(8,128)S(1)} %get-tuple-element.233, f32[32,768]{1,0:T(8,128)S(1)} %copy.12, f32[32,768]{1,0:T(8,128)S(1)} %get-tuple-element.251, f32[32,768]{1,0:T(8,128)S(1)} %get-tuple-element.266, f32[768]{0:T(1024)S(1)} %get-tuple-element.235, pred[]{:T(512)S(6)} %compare.3), kind=kOutput, calls=%fused_computation.6.clone.1 | convolution fusion | flops 226590720 | bytes 2755585 | tf_op jit(solution)/shard_map/while/body/eval_jaxpr/dot_general | solution.py:43
  53.5 0.0 collective-permute-done.1
  53.5 1.8 %collective-permute-done.2 = f32[32,768]{1,0:T(8,128)S(1)} collective-permute-done((f32[32,768]{1,0:T(8,128)S(1)}, f32[32,768]{1,0:T(8,128)S(1)}, u32[]{:S(2)}, u32[]{:S(2)}) %collective-permute-start.2) | collective-permute-done | bytes 98336 | tf_op jit(solution)/shard_map/while/body/eval_jaxpr/ppermute | solution.py:12
  55.3 0.0 collective-permute-done
  55.3 2.1 %fusion.15 = f32[768,768]{1,0:T(8,128)S(1)} fusion(f32[1,768]{1,0:T(1,128)S(1)} %get-tuple-element.280, f32[30,768]{1,0:T(8,128)S(1)} %maximum_multiply_fusion, f32[15,768]{1,0:T(8,128)S(1)} %get-tuple-element.169, f32[15,768]{1,0:T(8,128)S(1)} %get-tuple-element.168, f32[1,768]{1,0:T(1,128)S(1)} %slice.31), kind=kOutput, calls=%fused_computation.24 | convolution fusion | flops 219485952 | bytes 2549760 | tf_op jit(solution)/shard_map/dot_general | solution.py:35
  57.4 3.5 %fusion.24 = (f32[768]{0:T(1024)S(1)}, f32[768]{0:T(1024)S(1)}, f32[768,768]{1,0:T(8,128)S(1)}) fusion(f32[768,768]{1,0:T(8,128)S(1)} %fusion.15, f32[32,768]{1,0:T(8,128)S(1)} %get-tuple-element.271, f32[32,768]{1,0:T(8,128)S(1)} %get-tuple-element.109, f32[768]{0:T(1024)S(1)} %multiply_reduce_fusion.1, f32[768]{0:T(1024)S(1)} %get-tuple-element.283), kind=kOutput, calls=%fused_computation.40 | convolution fusion | flops 232978944 | bytes 4927488 | tf_op jit(solution)/shard_map/dot_general | solution.py:23
  60.9 1.4 %fusion.27 = f32[32,768]{1,0:T(8,128)S(1)} fusion(f32[32,768]{1,0:T(8,128)S(1)} %get-tuple-element.271, f32[768,768]{1,0:T(8,128)S(1)} %get-tuple-element.170), kind=kOutput, calls=%fused_computation.43 | convolution fusion | flops 226492416 | bytes 2555904 | tf_op jit(solution)/shard_map/dot_general | solution.py:50
  62.4 0.1 collective-permute-start.5
  62.4 2.2 %convolution_subtract_fusion = f32[32,768]{1,0:T(8,128)S(1)} fusion(f32[32,768]{1,0:T(8,128)S(1)} %get-tuple-element.109, f32[768,768]{1,0:T(8,128)S(1)} %get-tuple-element.170, f32[32,768]{1,0:T(8,128)S(1)} %get-tuple-element.271, f32[768]{0:T(1024)S(1)} %get-tuple-element.143), kind=kOutput, calls=%fused_computation.20 | convolution fusion | flops 226541568 | bytes 2657280 | tf_op jit(solution)/shard_map/dot_general | solution.py:43
  64.7 3.0 %collective-permute-done.5 = f32[32,768]{1,0:T(8,128)S(1)} collective-permute-done((f32[32,768]{1,0:T(8,128)S(1)}, f32[32,768]{1,0:T(8,128)S(1)}, u32[]{:S(2)}, u32[]{:S(2)}) %collective-permute-start.5) | collective-permute-done | bytes 98336 | tf_op jit(solution)/shard_map/ppermute | solution.py:12
  67.7 0.7 %add_multiply_fusion = f32[32,768]{1,0:T(8,128)} fusion(f32[32,768]{1,0:T(8,128)S(1)} %collective-permute-done.5, f32[32,768]{1,0:T(8,128)S(1)} %get-tuple-element.107, f32[32,768]{1,0:T(8,128)S(1)} %convolution_subtract_fusion, f32[32]{0:T(128)S(1)} %broadcast_divide_fusion.1), kind=kLoop, calls=%fused_computation.32 | loop fusion | flops 73728 | bytes 393344 | tf_op jit(solution)/shard_map/mul | solution.py:75
  (24 shorter events, 0.3 us)
Async XLA Ops:
  1.0 8.6 %collective-permute-start.3 = (f32[32,768]{1,0:T(8,128)S(1)}, f32[32,768]{1,0:T(8,128)S(1)}, u32[]{:S(2)}, u32[]{:S(2)}) collective-permute-start(f32[32,768]{1,0:T(8,128)S(1)} %get-tuple-element.244), channel_id=1, source_target_pairs={{0,15},{1,0},{2,1},{3,2},{4,3},{5,4},{6,5},{7,6},{8,7},{9,8},{10,9... | collective-permute-start | bytes 294920 | tf_op jit(solution)/shard_map/ppermute | solution.py:12
  2.6 7.0 %collective-permute-start.4 = (f32[31,768]{1,0:T(8,128)S(1)}, f32[31,768]{1,0:T(8,128)S(1)}, u32[]{:S(2)}, u32[]{:S(2)}) collective-permute-start(f32[31,768]{1,0:T(8,128)S(1)} %fusion.14), channel_id=1, source_target_pairs={{0,15},{1,0},{2,1},{3,2},{4,3},{5,4},{6,5},{7,6},{8,7},{9,8},{10,9... | collective-permute-start | bytes 285704 | tf_op jit(solution)/shard_map/ppermute | solution.py:12
  9.7 17.3 %collective-permute-start = (f32[32,768]{1,0:T(8,128)S(1)}, f32[32,768]{1,0:T(8,128)S(1)}, u32[]{:S(2)}, u32[]{:S(2)}) collective-permute-start(f32[32,768]{1,0:T(8,128)S(1)} %copy.12), channel_id=1, source_target_pairs={{0,15},{1,0},{2,1},{3,2},{4,3},{5,4},{6,5},{7,6},{8,7},{9,8},{10,9... | collective-permute-start | bytes 294920 | tf_op jit(solution)/shard_map/while/body/eval_jaxpr/ppermute | solution.py:12
  11.1 14.1 %collective-permute-start.1 = (f32[31,768]{1,0:T(8,128)S(1)}, f32[31,768]{1,0:T(8,128)S(1)}, u32[]{:S(2)}, u32[]{:S(2)}) collective-permute-start(f32[31,768]{1,0:T(8,128)S(1)} %copy.13), channel_id=1, source_target_pairs={{0,15},{1,0},{2,1},{3,2},{4,3},{5,4},{6,5},{7,6},{8,7},{9,8},{10,9... | collective-permute-start | bytes 285704 | tf_op jit(solution)/shard_map/while/body/eval_jaxpr/ppermute | solution.py:12
  22.9 4.1 %collective-permute-start.2 = (f32[32,768]{1,0:T(8,128)S(1)}, f32[32,768]{1,0:T(8,128)S(1)}, u32[]{:S(2)}, u32[]{:S(2)}) collective-permute-start(f32[32,768]{1,0:T(8,128)S(1)} %fusion.64), channel_id=1, source_target_pairs={{0,15},{1,0},{2,1},{3,2},{4,3},{5,4},{6,5},{7,6},{8,7},{9,8},{10,9... | collective-permute-start | bytes 294920 | tf_op jit(solution)/shard_map/while/body/eval_jaxpr/ppermute | solution.py:12
  27.0 14.1 %collective-permute-start = (f32[32,768]{1,0:T(8,128)S(1)}, f32[32,768]{1,0:T(8,128)S(1)}, u32[]{:S(2)}, u32[]{:S(2)}) collective-permute-start(f32[32,768]{1,0:T(8,128)S(1)} %copy.12), channel_id=1, source_target_pairs={{0,15},{1,0},{2,1},{3,2},{4,3},{5,4},{6,5},{7,6},{8,7},{9,8},{10,9... | collective-permute-start | bytes 294920 | tf_op jit(solution)/shard_map/while/body/eval_jaxpr/ppermute | solution.py:12
  27.1 12.3 %collective-permute-start.1 = (f32[31,768]{1,0:T(8,128)S(1)}, f32[31,768]{1,0:T(8,128)S(1)}, u32[]{:S(2)}, u32[]{:S(2)}) collective-permute-start(f32[31,768]{1,0:T(8,128)S(1)} %copy.13), channel_id=1, source_target_pairs={{0,15},{1,0},{2,1},{3,2},{4,3},{5,4},{6,5},{7,6},{8,7},{9,8},{10,9... | collective-permute-start | bytes 285704 | tf_op jit(solution)/shard_map/while/body/eval_jaxpr/ppermute | solution.py:12
  37.0 4.1 %collective-permute-start.2 = (f32[32,768]{1,0:T(8,128)S(1)}, f32[32,768]{1,0:T(8,128)S(1)}, u32[]{:S(2)}, u32[]{:S(2)}) collective-permute-start(f32[32,768]{1,0:T(8,128)S(1)} %fusion.64), channel_id=1, source_target_pairs={{0,15},{1,0},{2,1},{3,2},{4,3},{5,4},{6,5},{7,6},{8,7},{9,8},{10,9... | collective-permute-start | bytes 294920 | tf_op jit(solution)/shard_map/while/body/eval_jaxpr/ppermute | solution.py:12
  41.1 14.1 %collective-permute-start = (f32[32,768]{1,0:T(8,128)S(1)}, f32[32,768]{1,0:T(8,128)S(1)}, u32[]{:S(2)}, u32[]{:S(2)}) collective-permute-start(f32[32,768]{1,0:T(8,128)S(1)} %copy.12), channel_id=1, source_target_pairs={{0,15},{1,0},{2,1},{3,2},{4,3},{5,4},{6,5},{7,6},{8,7},{9,8},{10,9... | collective-permute-start | bytes 294920 | tf_op jit(solution)/shard_map/while/body/eval_jaxpr/ppermute | solution.py:12
  41.2 12.3 %collective-permute-start.1 = (f32[31,768]{1,0:T(8,128)S(1)}, f32[31,768]{1,0:T(8,128)S(1)}, u32[]{:S(2)}, u32[]{:S(2)}) collective-permute-start(f32[31,768]{1,0:T(8,128)S(1)} %copy.13), channel_id=1, source_target_pairs={{0,15},{1,0},{2,1},{3,2},{4,3},{5,4},{6,5},{7,6},{8,7},{9,8},{10,9... | collective-permute-start | bytes 285704 | tf_op jit(solution)/shard_map/while/body/eval_jaxpr/ppermute | solution.py:12
  51.2 4.1 %collective-permute-start.2 = (f32[32,768]{1,0:T(8,128)S(1)}, f32[32,768]{1,0:T(8,128)S(1)}, u32[]{:S(2)}, u32[]{:S(2)}) collective-permute-start(f32[32,768]{1,0:T(8,128)S(1)} %fusion.64), channel_id=1, source_target_pairs={{0,15},{1,0},{2,1},{3,2},{4,3},{5,4},{6,5},{7,6},{8,7},{9,8},{10,9... | collective-permute-start | bytes 294920 | tf_op jit(solution)/shard_map/while/body/eval_jaxpr/ppermute | solution.py:12
  62.4 5.3 %collective-permute-start.5 = (f32[32,768]{1,0:T(8,128)S(1)}, f32[32,768]{1,0:T(8,128)S(1)}, u32[]{:S(2)}, u32[]{:S(2)}) collective-permute-start(f32[32,768]{1,0:T(8,128)S(1)} %subtract_add_fusion), channel_id=1, source_target_pairs={{0,4},{1,5},{2,6},{3,7},{4,8},{5,9},{6,10},{7,11},{8,12},{9,13},{1... | collective-permute-start | bytes 294920 | tf_op jit(solution)/shard_map/ppermute | solution.py:12
where the time goes:
time: 68.7 us; the launch traced here: 68.4 us
  matrix products  37.2 us (54%)
  starting transfers between devices  17.5 us (25%)
  waiting for transfers between devices  8.39 us (12%)
  other arithmetic  4.19 us (6%)
  local copies, waits for them, and re-layouts  0.79 us (1%)
    ppermute x12, starting transfers between devices, shifted(): return lax.ppermute(value, axis, pairs)  17.5 us
    dot_general x4, matrix products, tile_terms(): lax.dot_general(own_scaled, vis_scaled, contract_first, precision=lax.Pre...  14.1 us
    dot_general x4, matrix products, tile_terms(): lax.dot_general(vis_scaled, weighted, (((1,), (1,)), ((), ())), precision...  8.87 us
    ppermute x12, waiting for transfers between devices, shifted(): return lax.ppermute(value, axis, pairs)  8.39 us
    dot_general x4, matrix products, tile_terms(): lax.dot_general(left_rows, right_rows, contract_first, precision=lax.Prec...  8.22 us
    dot_general x4, matrix products, tile_terms(): jnp.dot(own_scaled, weighted, precision=lax.Precision.HIGHEST, preferred_...  6.03 us
  transfers between devices with their start and end apart: 12, of which 4 were waited for; matrix products, arithmetic and copies ran while one was open for 49% of the time, Pallas kernels for 0%

commit v1 on v0

v1 whole, which is shorter than its diff:
```python
import functools
import math

import jax
import jax.numpy as jnp
from jax import lax
from jax.experimental import pallas as pl
from jax.experimental.pallas import tpu as pltpu
from jax.sharding import PartitionSpec as P

unit = 5.0**0.5 * math.log2(math.e)
ln_two = math.log(2.0)
inv_ln_two = 1.0 / ln_two
f32, bf16 = jnp.float32, jnp.bfloat16
row_chunk = 256
piece = 256


def pieces(x):
    high = x.astype(bf16)
    rest = x - high.astype(f32)
    mid = rest.astype(bf16)
    low = (rest - mid.astype(f32)).astype(bf16)
    return high, mid, low


def norm_rows(field, own):
    high, mid, low = (p.astype(f32) for p in pieces(jnp.sum(field * field, 0, keepdims=True)))
    row = lax.broadcasted_iota(jnp.int32, (16, field.shape[1]), 0)
    first = 0 if own else 3
    ones = (row >= 3 - first) & (row < 6 - first)
    out = jnp.where(ones, 1.0, 0.0)
    for at, piece in enumerate((high, mid, low)):
        out = jnp.where(row == first + at, piece, out)
    return out.astype(bf16)


def kernel(
    dims, steps, count, coords, alpha, solves, probes, lengths, out,
    msg, recv, left_d, left_c, right_d, right_c, acc, send_sem, recv_sem,
):
    me = lax.axis_index("blk")
    core = lax.rem(me, 2)
    side = lax.rem(me // 2, 2)
    partner = {"blk": me + 1 - 2 * core}
    mate = {"blk": me + 2 - 4 * side}
    rows, block = msg.shape
    width = (rows - dims) // 2
    msg[:dims, :] = coords[...]
    msg[dims : dims + width, :] = jnp.concatenate([solves[...], alpha[...]], 0)
    msg[dims + width :, :] = jnp.concatenate([probes[...], jnp.zeros_like(alpha)], 0)

    def at(offset):
        return {"blk": lax.rem(me + offset + count, count)}

    offsets = [sign * k for k in range(4, steps + 1, 4) for sign in (1, -1)]
    straight = {k: i for i, k in enumerate(offsets)}
    straights = len(offsets)
    rails = 2 * straights
    barrier = pltpu.get_barrier_semaphore()
    devices = [at(k) for k in offsets] + [mate, partner]
    for device in devices:
        pl.semaphore_signal(barrier, inc=1, device_id=device, device_id_type=pl.DeviceIdType.MESH)
    pl.semaphore_wait(barrier, len(devices))

    copies = {}
    parts = block // piece

    def send(src, slot, part, device):
        columns = pl.ds(part * piece, piece)
        copy = pltpu.make_async_remote_copy(
            src_ref=src.at[:, columns],
            dst_ref=recv.at[slot, :, columns],
            send_sem=send_sem.at[slot, part],
            recv_sem=recv_sem.at[slot, part],
            device_id=device,
            device_id_type=pl.DeviceIdType.MESH,
        )
        copy.start()
        copies[slot, part] = copy

    def arrive(slot, part):
        copies[slot, part].wait_recv()

    for part in range(parts):
        send(msg, rails, part, partner)
        for k in offsets:
            send(msg, straight[-k], part, at(k))
        send(msg, straights, part, mate)

    dim = lax.broadcasted_iota(jnp.int32, (dims, 128), 0)
    length = jnp.full((dims, 128), 1.0, f32)
    for d in range(dims):
        length = jnp.where(dim == d, lengths[d], length)
    length = length[:, :1]
    inverse = unit / length

    field = msg[:dims, :] * inverse
    high, mid, low = pieces(-2.0 * field)
    left_d[...] = jnp.concatenate([high, high, high, norm_rows(field, True), mid, mid, low], 0).T
    row = lax.broadcasted_iota(jnp.int32, (width, block), 0)
    scale = -ln_two / (2.0 * (width - 1))
    top, bottom = msg[dims : dims + width, :], msg[dims + width :, :]
    first = jnp.where(row == width - 1, ln_two * top, scale * bottom)
    second = jnp.where(row == width - 1, 0.0, scale * top)
    high, mid, low = pieces(jnp.concatenate([first, second], 0))
    left_c[...] = jnp.concatenate([high, high, high, mid, mid, low], 0).T

    done = [0]

    def visit(slot, part):
        buffer, fresh = done[0] % 2, done[0] == 0
        done[0] += 1
        columns = pl.ds(part * piece, piece)
        field = recv[slot, :dims, columns] * inverse
        high, mid, low = pieces(field)
        right_d[buffer] = jnp.concatenate([high, mid, low, norm_rows(field, False), high, mid, high], 0)
        table = recv[slot, dims:, columns]
        high, mid, low = pieces(table)
        right_c[buffer] = jnp.concatenate([high, mid, low, high, mid, high], 0)
        across = right_d[buffer, : 3 * dims + 16, :]
        for start in range(0, block, row_chunk):
            lines = pl.ds(start, row_chunk)
            distance = jnp.dot(left_d[lines, :], right_d[buffer], preferred_element_type=f32)
            coupling = jnp.dot(left_c[lines, :], right_c[buffer], preferred_element_type=f32)
            distance = jnp.maximum(distance, 1e-30)
            radius = distance * lax.rsqrt(distance)
            weighted = coupling * ((radius + inv_ln_two) * jnp.exp2(-radius))
            w_high = weighted.astype(bf16)
            w_low = (weighted - w_high.astype(f32)).astype(bf16)
            contract = (((1,), (1,)), ((), ()))
            part_sum = lax.dot_general(w_high, across, contract, preferred_element_type=f32)
            part_sum += lax.dot_general(w_low, across, contract, preferred_element_type=f32)
            if fresh and part == 0:
                acc[lines, :] = part_sum
            else:
                acc[lines, :] += part_sum

    every = range(parts)
    for part in every:
        arrive(rails, part)
        visit(rails, part)

    mated, crossed = straights, rails
    for k in range(4, steps + 1, 4):
        plus, minus = straight[k], straight[-k]
        last = k == steps
        for part in every:
            if k == 4:
                arrive(straights, part)
                send(recv.at[straights], rails + 1, part, partner)
                visit(straights, part)
            arrive(plus, part)
            arrive(minus, part)
            if last:
                send(recv.at[plus + side], straights + 1 + plus, part, mate)
                send(recv.at[plus + core], rails + 2 + plus, part, partner)
            else:
                for slot in (plus, minus):
                    send(recv.at[slot], straights + 1 + slot, part, mate)
                    send(recv.at[slot], rails + 2 + slot, part, partner)
            if k == 4:
                arrive(rails + 1, part)
                visit(rails + 1, part)
            visit(plus, part)
            visit(minus, part)
    ends = rails + 1 + straights
    for slot in range(straights + 1, rails):
        for part in every:
            arrive(slot, part)
            send(recv.at[slot], ends + slot - straights - 1, part, partner)
            arrive(rails + 1 + slot - straights, part)
            visit(rails + 1 + slot - straights, part)
            visit(slot, part)
    for slot in range(ends, 2 * rails):
        for part in every:
            arrive(slot, part)
            visit(slot, part)
    total = acc[...].T
    moved = total[:dims] + total[dims : 2 * dims] + total[2 * dims : 3 * dims]
    field = msg[:dims, :] * inverse
    out[...] = (-(5.0 / 3.0) / unit / length) * (field * total[3 * dims : 3 * dims + 1] - moved)
    for copy in copies.values():
        copy.wait_send()


def on_device(coords, alpha, probe_solves, probes, lengthscale):
    count = lax.axis_size("blk")
    steps = count // 4
    dims, block = coords.shape
    table_rows = 2 * (probes.shape[0] + 1)
    rows = dims + table_rows
    depth_d, depth_c = 6 * dims + 16, 6 * table_rows
    parts = block // piece
    return pl.pallas_call(
        functools.partial(kernel, dims, steps, count),
        out_shape=jax.ShapeDtypeStruct((dims, block), f32),
        in_specs=[pl.BlockSpec(memory_space=pltpu.VMEM)] * 4 + [pl.BlockSpec(memory_space=pltpu.SMEM)],
        out_specs=pl.BlockSpec(memory_space=pltpu.VMEM),
        scratch_shapes=[
            pltpu.VMEM((rows, block), f32),
            pltpu.VMEM((2 * steps, rows, block), f32),
            pltpu.VMEM((block, depth_d), bf16),
            pltpu.VMEM((block, depth_c), bf16),
            pltpu.VMEM((2, depth_d, piece), bf16),
            pltpu.VMEM((2, depth_c, piece), bf16),
            pltpu.VMEM((block, 3 * dims + 16), f32),
            pltpu.SemaphoreType.DMA((2 * steps, parts)),
            pltpu.SemaphoreType.DMA((2 * steps, parts)),
        ],
        compiler_params=pltpu.CompilerParams(collective_id=0, has_side_effects=True),
    )(coords, alpha[None], probe_solves, probes, lengthscale)


def solution(mesh):
    return jax.shard_map(
        on_device,
        mesh=mesh,
        in_specs=(
            P(None, ("groups", "blk")),
            P(("groups", "blk")),
            P(None, ("groups", "blk")),
            P(None, ("groups", "blk")),
            P(),
        ),
        out_specs=P(None, ("groups", "blk")),
        check_vma=False,
    )
```

time: 68.7 us -> 32.4 us (0.47)
  matrix products: 37.2 us -> 0 us
  Pallas kernels: 0 us -> 29.2 us
  starting transfers between devices: 17.5 us -> 0 us
  waiting for transfers between devices: 8.39 us -> 0 us
  other arithmetic: 4.19 us -> 0 us
  local copies, waits for them, and re-layouts: 0.79 us -> 2.81 us
    dot_general x16 -> x0, matrix products: 37.2 us -> none  [the longest x4 14.1 us: tile_terms(): lax.dot_general(own_scaled, vis_scaled, contract_first, precision=lax.Pre...]
    pallas_call x0 -> x1, Pallas kernels: none -> 29.2 us  [on_device(): pl.pallas_call(functools.partial(kernel, dims, steps, count), out_shape=j...]
    ppermute x12 -> x0, starting transfers between devices: 17.5 us -> none  [shifted(): return lax.ppermute(value, axis, pairs)]
    ppermute x12 -> x0, waiting for transfers between devices: 8.39 us -> none  [shifted(): return lax.ppermute(value, axis, pairs)]
    mul x5 -> x0, other arithmetic: 1.6 us -> none  [the longest x4 0.89 us: tile_terms(): left_rows = jnp.concatenate([own_table[:1], -half_inv * own_table[1:]], 0)]
    unnamed x0 -> x1, local copies, waits for them, and re-layouts: none -> 1.54 us
    reduce_sum x5 -> x0, other arithmetic: 1.07 us -> none  [the longest x1 0.99 us: tile_terms(): own_square = jnp.sum(own_scaled * own_scaled, 0)]
    concatenate x1 -> x0, other arithmetic: 0.84 us -> none  [on_device(): table = jnp.concatenate([alpha[None], probe_solves, probes], 0)]
  transfers between devices with their start and end apart: 12 -> 0, of which waited for: 4 -> 0; matrix products, arithmetic and copies ran while one was open for 49% -> 0% of each run, Pallas kernels for 0% -> 0%
where the time goes in v1:
time: 32.4 us; the launch traced here: 32 us
  Pallas kernels  29.2 us (90%)
  local copies, waits for them, and re-layouts  2.81 us (9%)
    pallas_call x1, Pallas kernels, on_device(): pl.pallas_call(functools.partial(kernel, dims, steps, count), out_shape=j...  29.2 us
    unnamed x1, local copies, waits for them, and re-layouts  1.54 us
    broadcast_in_dim x1, local copies, waits for them, and re-layouts, on_device(): alpha[None]  1.27 us

profile of v1, /device:TPU:1, one launch (start us, length us, event | category | flops | bytes accessed | tf_op | source)
XLA Modules:
  0.0 32.0 jit_solution(16662784045233628001)
XLA Ops:
  0.0 1.3 %broadcast_in_dim.3.alpha = f32[1,768]{1,0:T(1,128)} reshape(f32[768]{0:T(1024)} %param.6) | data formatting | bytes 6144 | tf_op jit(solution)/shard_map/broadcast_in_dim | solution.py:212
  1.3 29.2 %shard_map.55 = f32[32,768]{1,0:T(8,128)} custom-call(f32[32,768]{1,0:T(8,128)} %coords.1, f32[1,768]{1,0:T(1,128)} %broadcast_in_dim.3.alpha, f32[15,768]{1,0:T(8,128)} %solves.1, f32[15,768]{1,0:T(8,128)} %probes.1, f32[32]{0:T(128)} %lengths.1), custom_call_target="tpu_custom_call" | custom-call | tf_op jit(solution)/shard_map/pallas_call | solution.py:195
  30.5 1.5 %copy.7 = f32[32,768]{1,0:T(8,128)} copy(f32[32,768]{1,0:T(8,128)} %shard_map.55) | data formatting | bytes 196608

commit v2 on v1

--- a/solution.py
+++ b/solution.py
@@ -12,7 +12,6 @@
 ln_two = math.log(2.0)
 inv_ln_two = 1.0 / ln_two
 f32, bf16 = jnp.float32, jnp.bfloat16
-row_chunk = 256
 piece = 256
 
 
@@ -47,8 +46,9 @@
     rows, block = msg.shape
     width = (rows - dims) // 2
     msg[:dims, :] = coords[...]
-    msg[dims : dims + width, :] = jnp.concatenate([solves[...], alpha[...]], 0)
-    msg[dims + width :, :] = jnp.concatenate([probes[...], jnp.zeros_like(alpha)], 0)
+    line = alpha[...].reshape(1, block)
+    msg[dims : dims + width, :] = jnp.concatenate([solves[...], line], 0)
+    msg[dims + width :, :] = jnp.concatenate([probes[...], jnp.zeros_like(line)], 0)
 
     def at(offset):
         return {"blk": lax.rem(me + offset + count, count)}
@@ -119,8 +119,8 @@
         high, mid, low = pieces(table)
         right_c[buffer] = jnp.concatenate([high, mid, low, high, mid, high], 0)
         across = right_d[buffer, : 3 * dims + 16, :]
-        for start in range(0, block, row_chunk):
-            lines = pl.ds(start, row_chunk)
+        for start in (0,):
+            lines = pl.ds(start, block)
             distance = jnp.dot(left_d[lines, :], right_d[buffer], preferred_element_type=f32)
             coupling = jnp.dot(left_c[lines, :], right_c[buffer], preferred_element_type=f32)
             distance = jnp.maximum(distance, 1e-30)
@@ -209,7 +209,7 @@
             pltpu.SemaphoreType.DMA((2 * steps, parts)),
         ],
         compiler_params=pltpu.CompilerParams(collective_id=0, has_side_effects=True),
-    )(coords, alpha[None], probe_solves, probes, lengthscale)
+    )(coords, alpha, probe_solves, probes, lengthscale)
 
 
 def solution(mesh):

time: 32.4 us -> 27.6 us (0.85)
  Pallas kernels: 29.2 us -> 25.8 us
  local copies, waits for them, and re-layouts: 2.81 us -> 1.54 us
    pallas_call x1, Pallas kernels: 29.2 us -> 25.8 us  [on_device(): pl.pallas_call(functools.partial(kernel, dims, steps, count), out_shape=j...]
    broadcast_in_dim x1 -> x0, local copies, waits for them, and re-layouts: 1.27 us -> none  [on_device(): alpha[None]]
where the time goes in v2:
time: 27.6 us; the launch traced here: 27.4 us
  Pallas kernels  25.8 us (93%)
  local copies, waits for them, and re-layouts  1.54 us (6%)
    pallas_call x1, Pallas kernels, on_device(): pl.pallas_call(functools.partial(kernel, dims, steps, count), out_shape=j...  25.8 us
    unnamed x1, local copies, waits for them, and re-layouts  1.54 us

profile of v2, /device:TPU:1, one launch (start us, length us, event | category | flops | bytes accessed | tf_op | source)
XLA Modules:
  0.0 27.4 jit_solution(8077684097401309976)
XLA Ops:
  0.0 25.8 %shard_map.55 = f32[32,768]{1,0:T(8,128)} custom-call(f32[32,768]{1,0:T(8,128)} %coords.1, f32[768]{0:T(1024)} %alpha.1, f32[15,768]{1,0:T(8,128)} %solves.1, f32[15,768]{1,0:T(8,128)} %probes.1, f32[32]{0:T(128)} %lengths.1), custom_call_target="tpu_custom_call" | custom-call | tf_op jit(solution)/shard_map/pallas_call | solution.py:195
  25.8 1.5 %copy.7 = f32[32,768]{1,0:T(8,128)} copy(f32[32,768]{1,0:T(8,128)} %shard_map.55) | data formatting | bytes 196608
